TPU v7x, 128 devices: a whole 4x4x4 slice. The times are simulated.
128 devices in a mesh: branch: 4 (over z_lo, core), shard: 32 (over y, x, z_hi).
Axes of the slice: x: 4, y: 4, z: 4 (z_hi: 2, z_lo: 2; z = z_hi * 2 + z_lo), core: 2. Of those that a mesh axis runs over, the one named last changes fastest.
Arguments:
- attention_weights: bfloat16 [4, 2, 4096, 4096], P('branch', None, None, 'shard'), may hold values from -1.25 to 1.25
- ffn_weights: bfloat16 [4, 3, 4096, 11008], P('branch', None, 'shard'), may hold values from -0.3125 to 0.3125
- tokens: bfloat16 [2048, 4096], P(('branch', 'shard')), may hold values from -6 to 6
- routes: int32 [2048, 2], P(('branch', 'shard')), may hold values from 0 to 3, all different within a row; in each aligned block of 16 rows (0 to 15, 16 to 31, ...) at most 12 rows name the same one
- router: bfloat16 [4096, 4], replicated, may hold values from -0.09375 to 0.09375
Outputs:
- merged_attention: bfloat16 [2, 4096, 4096], P(None, 'branch', 'shard')
- expert_weights: bfloat16 [4, 3, 4096, 11008], P('branch', None, None, 'shard')
- mixed_output: bfloat16 [2048, 4096], P(('branch', 'shard'))
Inputs may be any that keep to these rules, and one draw needn't show every extreme that they name: `routes`: the 2 experts of a row differ. In each aligned block of 16 rows (the rows of one device) no expert is named by more than 12 rows, and in some blocks one expert is named by exactly 12 rows.
All inputs are finite; a program needn't handle non-finite values.
Results may differ from a plain program's by a relative error of at most 0.018.
Values may be sent and summed in bfloat16 or wider, within the bound.
A program may use at most 192 MiB of HBM per device.

v0:
```python
import jax
import jax.numpy as jnp
from jax import lax
from jax.sharding import Mesh
from jax.sharding import PartitionSpec as P

SHARD = ("shard_0", "shard_1", "shard_2")
BRANCH_SHARD = ("branch", "shard_0", "shard_1", "shard_2")


def own_rows(terms, axes):
    running = terms.astype(jnp.bfloat16)
    for axis in axes:
        running = lax.psum_scatter(running, axis, scatter_dimension=0, tiled=True)
    return running.astype(jnp.float32)


def slot_table(route_rows, experts_count, capacity):
    chosen = (route_rows[:, :, None] == jnp.arange(experts_count, dtype=jnp.int32)).astype(
        jnp.int32
    )
    flat_picks = chosen.reshape(-1, experts_count)
    before = jnp.cumsum(flat_picks, axis=0) - flat_picks
    position = jnp.sum(before * flat_picks, axis=1)
    slot_id = route_rows.reshape(-1) * capacity + position
    one_hot = (slot_id[:, None] == jnp.arange(experts_count * capacity, dtype=jnp.int32)).astype(
        jnp.float32
    )
    return jnp.sum(one_hot.reshape(route_rows.shape[0], route_rows.shape[1], -1), axis=1)


def local(attention_weights, ffn_weights, tokens, routes, router):
    branches = lax.axis_size("branch")
    expert_weights = lax.all_to_all(ffn_weights, SHARD, split_axis=3, concat_axis=2, tiled=True)
    gate_weight = expert_weights[0, 0]
    up_weight = expert_weights[0, 1]
    down_weight = expert_weights[0, 2]
    tok_count = tokens.shape[0]
    model_width = tokens.shape[1]
    capacity = 3 * tok_count // 4
    slot_map = slot_table(routes, branches, capacity)
    buffers = lax.dot_general(
        slot_map.astype(jnp.bfloat16),
        tokens,
        (((0,), (0,)), ((), ())),
        preferred_element_type=jnp.float32,
    )
    buffers = buffers.astype(jnp.bfloat16).reshape(branches, capacity, model_width)
    arrived = lax.all_to_all(buffers, "branch", split_axis=0, concat_axis=0, tiled=True)
    slot_rows = lax.all_gather(
        arrived.reshape(branches * capacity, model_width), SHARD, axis=0, tiled=True
    )
    gate_proj = jnp.dot(slot_rows, gate_weight, preferred_element_type=jnp.float32)
    up_proj = jnp.dot(slot_rows, up_weight, preferred_element_type=jnp.float32)
    hidden = (jax.nn.silu(gate_proj) * up_proj).astype(jnp.bfloat16)
    summed = own_rows(
        lax.dot_general(
            hidden, down_weight, (((1,), (1,)), ((), ())), preferred_element_type=jnp.float32
        ),
        SHARD,
    )
    outputs = summed.astype(jnp.bfloat16).reshape(branches, capacity, model_width)
    returned = lax.all_to_all(outputs, "branch", split_axis=0, concat_axis=0, tiled=True)
    gates_all = jax.nn.sigmoid(jnp.dot(tokens, router, preferred_element_type=jnp.float32))
    weighting = slot_map * jnp.repeat(gates_all, capacity, axis=1)
    mixed_output = jnp.dot(
        weighting, returned.reshape(branches * capacity, model_width).astype(jnp.float32)
    )
    mixed_output = mixed_output.astype(jnp.bfloat16)
    traded = lax.all_to_all(attention_weights, "branch", split_axis=2, concat_axis=0, tiled=True)
    summed_attention = jnp.sum(traded.astype(jnp.float32), axis=0)
    merged_attention = (summed_attention * (1.0 / branches)).astype(jnp.bfloat16)
    return (merged_attention, expert_weights, mixed_output)


def solution(mesh):
    torus = Mesh(
        mesh.devices.reshape(mesh.shape["branch"], 4, 4, 2),
        ("branch", "shard_0", "shard_1", "shard_2"),
    )
    in_specs = (
        P("branch", None, None, SHARD),
        P("branch", None, SHARD, None),
        P(BRANCH_SHARD, None),
        P(BRANCH_SHARD, None),
        P(),
    )
    out_specs = (P(None, "branch", SHARD), P("branch", None, None, SHARD), P(BRANCH_SHARD, None))
    return jax.shard_map(local, mesh=torus, in_specs=in_specs, out_specs=out_specs, check_vma=False)
```

profile of v0, /device:TPU:1, one launch (start us, length us, event | category | flops | bytes accessed | tf_op | source)
XLA Modules:
  0.0 518.2 jit_solution(2717877055317344785)
XLA Ops:
  7.2 0.0 copy-start
  7.2 0.0 all-gather.2.cloned.1.call-start
  7.2 0.8 copy.58
  8.0 0.1 eq.30
  8.1 0.1 fusion.13
  8.2 0.1 reduce_window_sum.11
  8.2 0.2 select_reduce_fusion
  8.4 0.1 reduce_sum.33
  8.5 0.1 copy.59
  8.6 0.7 multiply_add_fusion
  9.3 0.1 convert_reduce_fusion.1
  9.4 0.0 copy-done
  9.4 0.3 convolution_convert_fusion.1
  9.7 0.1 reshape.45
  9.8 12.2 %all_to_all.37 = bf16[4,12,4096]{2,1,0:T(8,128)(2,1)S(1)} all-to-all(bf16[4,12,4096]{2,1,0:T(8,128)(2,1)S(1)} %reshape.45), channel_id=1, replica_groups=mesh['branch'=4,'shard_0'=4,'shard_1'=4,'shard_2'=2] {'branch'}, dimensions={0} | all-to-all | bytes 786432 | tf_op jit(solution)/shard_map/all_to_all | solution.py:49
  22.0 0.8 reshape.46
  22.8 0.0 all-gather.2.cloned.1.call-update
  22.9 0.0 reduce-scatter.4.cloned.1.call-start
  22.9 17.6 %copy.55 = bf16[1,3,128,11008]{2,1,0,3:T(4,128)(2,1)} copy(bf16[1,3,128,11008]{3,2,1,0:T(8,128)(2,1)} %param.6) | data formatting | bytes 16908288 | tf_op args[1]
  40.5 145.7 %all_to_all.38 = bf16[1,3,128,11008]{2,1,0,3:T(4,128)(2,1)S(1)} all-to-all(bf16[1,3,128,11008]{2,1,0,3:T(4,128)(2,1)} %copy.55), channel_id=1, replica_groups=mesh['branch'=4,'shard_0'=4,'shard_1'=4,'shard_2'=2] {'shard_0','shard_1..., dimensions={3} | all-to-all | bytes 16908288 | tf_op jit(solution)/shard_map/all_to_all | solution.py:34
  186.2 5.0 copy.56
  191.3 9.2 %copy.67 = bf16[1,3,32,43,8,128]{5,4,2,3,1,0:T(8,128)(2,1)} copy(bf16[1,3,32,43,8,128]{5,4,3,2,1,0:T(8,128)(2,1)} %bitcast.32) | data formatting | bytes 16908288 | tf_op jit(solution)/shard_map/all_to_all | solution.py:34
  200.4 67.3 %all-gather.2.cloned.1.call-done = bf16[1536,4096]{1,0:T(8,128)(2,1)} async-done(((bf16[48,4096]{1,0:T(8,128)(2,1)}), bf16[1536,4096]{1,0:T(8,128)(2,1)}) %all-gather.2.cloned.1.call-update) | async-done | bytes 12582928 | tf_op jit(solution)/shard_map/all_gather | solution.py:50
  267.7 8.5 %fusion.1 = f32[1536,344]{0,1:T(8,128)S(1)} fusion(bf16[1536,4096]{1,0:T(8,128)(2,1)} %all-gather.2.cloned.1.call-done, bf16[1,3,4096,344]{2,3,1,0:T(8,128)(2,1)} %bitcast.33), kind=kOutput, calls=%fused_computation.10 | convolution fusion | flops 4328521728 | bytes 17514496 | tf_op jit(solution)/shard_map/dot_general | solution.py:53
  276.2 21.6 %convolution_convert_fusion = bf16[1536,4096]{1,0:T(8,128)(2,1)} fusion(bf16[1,3,4096,344]{2,3,1,0:T(8,128)(2,1)} %bitcast.34, bf16[1536,4096]{1,0:T(8,128)(2,1)} %all-gather.2.cloned.1.call-done, f32[1536,344]{0,1:T(8,128)S(1)} %fusion.1), kind=kOutput, calls=%fused_computation | convolution fusion | flops 8666505216 | bytes 32915456 | tf_op jit(solution)/shard_map/dot_general | solution.py:57
  297.7 0.0 reduce-scatter.4.cloned.1.call-update
  297.7 0.0 copy-start.1
  297.8 0.0 reduce-scatter.6.cloned.1.call-start
  297.8 113.0 %reduce-scatter.4.cloned.1.call-done = bf16[384,4096]{1,0:T(8,128)(2,1)} async-done(((bf16[1536,4096]{1,0:T(8,128)(2,1)}), bf16[384,4096]{1,0:T(8,128)(2,1)}) %reduce-scatter.4.cloned.1.call-update) | async-done | bytes 3145744 | tf_op jit(solution)/shard_map/reduce_scatter | solution.py:14
  410.8 0.0 reduce-scatter.6.cloned.1.call-update
  410.8 0.2 reduce-scatter.8.cloned.1.call-start
  411.0 40.1 %reduce-scatter.6.cloned.1.call-done = bf16[96,4096]{1,0:T(8,128)(2,1)} async-done(((bf16[384,4096]{1,0:T(8,128)(2,1)}), bf16[96,4096]{1,0:T(8,128)(2,1)}) %reduce-scatter.6.cloned.1.call-update) | async-done | bytes 786448 | tf_op jit(solution)/shard_map/reduce_scatter | solution.py:14
  451.2 0.0 reduce-scatter.8.cloned.1.call-update
  451.2 0.0 copy-done.1
  451.2 18.1 %copy.54 = bf16[1,2,4096,128]{3,1,0,2:T(2,128)(2,1)} copy(bf16[1,2,4096,128]{3,2,1,0:T(8,128)(2,1)S(1)} %copy-done.1) | data formatting | bytes 4194304 | tf_op args[0]
  469.3 0.0 copy-start.2
  469.3 4.4 all-to-all-start
  473.8 0.1 reduce_sum.35
  473.8 0.0 copy-done.2
  473.9 0.2 fusion.10
  474.0 0.1 copy.60
  474.1 0.1 broadcast_multiply_fusion
  474.2 0.5 reduce-scatter.8.cloned.1.call-done
  474.8 1.9 reshape.47
  476.6 21.8 %all-to-all-done = bf16[1,2,4096,128]{3,1,0,2:T(2,128)(2,1)S(1)} async-done(((bf16[1,2,4096,128]{3,1,0,2:T(2,128)(2,1)}), bf16[1,2,4096,128]{3,1,0,2:T(2,128)(2,1)S(1)}, u32[]{:S(2)}, u32[]{:S(2)}) %all-to-all-start) | async-done | bytes 2097184 | tf_op jit(solution)/shard_map/all_to_all | solution.py:70
  498.5 4.4 all-to-all-start.3
  502.9 2.1 convert_reduce_fusion
  505.0 0.5 multiply_convert_fusion
  505.5 0.9 copy.62
  506.3 4.4 all-to-all-done.3
  510.7 1.0 fusion
Async XLA Ops:
  7.2 2.2 copy-start
  7.2 260.5 %all-gather.2.cloned.1.call-start = ((), (), s32[]{:S(2)}) async-start(), calls=%async_computation.7 | async-start | bytes 12976128 | tf_op jit(solution)/shard_map/all_gather | solution.py:50
  22.9 387.9 %reduce-scatter.4.cloned.1.call-start = ((), (), s32[]{:S(2)}) async-start(), calls=%async_computation.8 | async-start | bytes 15728640 | tf_op jit(solution)/shard_map/reduce_scatter | solution.py:14
  297.7 153.4 %copy-start.1 = (bf16[1,2,4096,128]{3,2,1,0:T(8,128)(2,1)S(1)}, bf16[1,2,4096,128]{3,2,1,0:T(8,128)(2,1)}, u32[]{:S(2)}) copy-start(bf16[1,2,4096,128]{3,2,1,0:T(8,128)(2,1)} %param.5) | copy-start | bytes 6291460
  297.8 153.4 %reduce-scatter.6.cloned.1.call-start = ((), (), s32[]{:S(2)}) async-start(), calls=%async_computation.9 | async-start | bytes 3932160 | tf_op jit(solution)/shard_map/reduce_scatter | solution.py:14
  410.8 64.0 %reduce-scatter.8.cloned.1.call-start = ((), (), s32[]{:S(2)}) async-start(), calls=%async_computation.10 | async-start | bytes 1179648 | tf_op jit(solution)/shard_map/reduce_scatter | solution.py:14
  469.3 4.5 copy-start.2
  469.3 29.1 %all-to-all-start = ((bf16[1,2,4096,128]{3,1,0,2:T(2,128)(2,1)}), bf16[1,2,4096,128]{3,1,0,2:T(2,128)(2,1)S(1)}, u32[]{:S(2)}, u32[]{:S(2)}) async-start(bf16[1,2,4096,128]{3,1,0,2:T(2,128)(2,1)} %copy.54), calls=%async_computation | async-start | bytes 4194304 | tf_op jit(solution)/shard_map/all_to_all | solution.py:70
  498.5 12.3 %all-to-all-start.3 = ((bf16[4,12,4096]{2,1,0:T(8,128)(2,1)}), bf16[4,12,4096]{2,1,0:T(8,128)(2,1)S(1)}, u32[]{:S(2)}, u32[]{:S(2)}) async-start(bf16[4,12,4096]{2,1,0:T(8,128)(2,1)} %reshape.47), calls=%async_computation.6 | async-start | bytes 1048576 | tf_op jit(solution)/shard_map/all_to_all | solution.py:63
Sparse Core Ops, SparseCore 0:
  23.0 244.6 all-gather.1
  297.9 112.8 reduce-scatter.3
  413.2 37.9 reduce-scatter.5
  453.4 21.3 reduce-scatter.7
where the time goes:
time: 519 us; the launch traced here: 518 us
  waiting for transfers between devices  247 us (48%)
  blocking collectives  158 us (30%)
  local copies, waits for them, and re-layouts  54.8 us (11%)
  matrix products  31.4 us (6%)
  between operations  13.9 us (3%)
  starting transfers between devices  9.18 us (2%)
    reduce_scatter x3, waiting for transfers between devices, own_rows(): running = lax.psum_scatter(running, axis, scatter_dimension=0, tiled=True)  154 us
    all_to_all x1, blocking collectives, local(): lax.all_to_all(ffn_weights, SHARD, split_axis=3, concat_axis=2, tiled=True)  146 us
    all_gather x1, waiting for transfers between devices, local(): lax.all_gather(arrived.reshape(branches * capacity, model_width), SHARD,...  67.3 us
    unnamed x10, local copies, waits for them, and re-layouts  37.4 us
    all_to_all x1, waiting for transfers between devices, local(): lax.all_to_all(attention_weights, 'branch', split_axis=2, concat_axis=0,...  21.8 us
    dot_general x1, matrix products, local(): lax.dot_general(hidden, down_weight, (((1,), (1,)), ((), ())), preferred_...  21.6 us
    all_to_all x2, local copies, waits for them, and re-layouts, local(): lax.all_to_all(ffn_weights, SHARD, split_axis=3, concat_axis=2, tiled=True)  14.2 us
    all_to_all x1, blocking collectives, local(): lax.all_to_all(buffers, 'branch', split_axis=0, concat_axis=0, tiled=True)  12.2 us
  transfers between devices with their start and end apart: 6, of which 6 were waited for; matrix products, arithmetic and copies ran while one was open for 11% of the time, Pallas kernels for 0%

commit v1 on v0

--- a/solution.py
+++ b/solution.py
@@ -3,9 +3,16 @@
 from jax import lax
 from jax.sharding import Mesh
 from jax.sharding import PartitionSpec as P
+from jax.lax import all_to_all, axis_size
 
 SHARD = ("shard_0", "shard_1", "shard_2")
 BRANCH_SHARD = ("branch", "shard_0", "shard_1", "shard_2")
+follow_threads = lambda array_here: jnp.concatenate(
+    all_to_all(
+        jnp.stack([array_here] * axis_size(SHARD)), axis_name=SHARD, split_axis=0, concat_axis=0
+    ),
+    axis=0,
+)
 
 
 def own_rows(terms, axes):
@@ -47,9 +54,7 @@
     )
     buffers = buffers.astype(jnp.bfloat16).reshape(branches, capacity, model_width)
     arrived = lax.all_to_all(buffers, "branch", split_axis=0, concat_axis=0, tiled=True)
-    slot_rows = lax.all_gather(
-        arrived.reshape(branches * capacity, model_width), SHARD, axis=0, tiled=True
-    )
+    slot_rows = follow_threads(arrived.reshape(branches * capacity, model_width))
     gate_proj = jnp.dot(slot_rows, gate_weight, preferred_element_type=jnp.float32)
     up_proj = jnp.dot(slot_rows, up_weight, preferred_element_type=jnp.float32)
     hidden = (jax.nn.silu(gate_proj) * up_proj).astype(jnp.bfloat16)

time: 519 us -> 728 us (1.40)
  waiting for transfers between devices: 247 us -> 556 us
  blocking collectives: 158 us -> 0 us
  starting transfers between devices: 9.18 us -> 57.3 us
  local copies, waits for them, and re-layouts: 54.8 us -> 64.6 us
    all_to_all x0 -> x3, waiting for transfers between devices: none -> 347 us  [the longest x1 175 us: local(): lax.all_to_all(ffn_weights, SHARD, split_axis=3, concat_axis=2, tiled=True)]
    all_to_all x2 -> x0, blocking collectives: 158 us -> none  [the longest x1 146 us: local(): lax.all_to_all(ffn_weights, SHARD, split_axis=3, concat_axis=2, tiled=True)]
    all_gather x1 -> x0, waiting for transfers between devices: 67.3 us -> none  [local(): lax.all_gather(arrived.reshape(branches * capacity, model_width), SHARD,...]
    all_to_all x0 -> x3, starting transfers between devices: none -> 47.9 us  [the longest x1 32.5 us: all_to_all(jnp.stack([array_here] * axis_size(SHARD)), axis_name=SHARD, s...]
    reduce_scatter x3, waiting for transfers between devices: 154 us -> 183 us  [own_rows(): running = lax.psum_scatter(running, axis, scatter_dimension=0, tiled=True)]
  transfers between devices with their start and end apart: 6 -> 8, of which waited for: 6 -> 7; matrix products, arithmetic and copies ran while one was open for 11% -> 8% of each run, Pallas kernels for 0% -> 0%
where the time goes in v1:
time: 728 us; the launch traced here: 727 us
  waiting for transfers between devices  556 us (76%)
  local copies, waits for them, and re-layouts  64.6 us (9%)
  starting transfers between devices  57.3 us (8%)
  matrix products  31.4 us (4%)
  between operations  13.9 us (2%)
    reduce_scatter x3, waiting for transfers between devices, own_rows(): running = lax.psum_scatter(running, axis, scatter_dimension=0, tiled=True)  183 us
    all_to_all x1, waiting for transfers between devices, local(): lax.all_to_all(ffn_weights, SHARD, split_axis=3, concat_axis=2, tiled=True)  175 us
    all_to_all x1, waiting for transfers between devices, all_to_all(jnp.stack([array_here] * axis_size(SHARD)), axis_name=SHARD, s...  172 us
    unnamed x10, local copies, waits for them, and re-layouts  37.3 us
    all_to_all x1, starting transfers between devices, all_to_all(jnp.stack([array_here] * axis_size(SHARD)), axis_name=SHARD, s...  32.5 us
    all_to_all x1, waiting for transfers between devices, local(): lax.all_to_all(attention_weights, 'branch', split_axis=2, concat_axis=0,...  21.7 us
    dot_general x1, matrix products, local(): lax.dot_general(hidden, down_weight, (((1,), (1,)), ((), ())), preferred_...  21.6 us
    all_to_all x2, local copies, waits for them, and re-layouts, local(): lax.all_to_all(ffn_weights, SHARD, split_axis=3, concat_axis=2, tiled=True)  17.9 us
  transfers between devices with their start and end apart: 8, of which 7 were waited for; matrix products, arithmetic and copies ran while one was open for 8% of the time, Pallas kernels for 0%

profile of v1, /device:TPU:1, one launch (start us, length us, event | category | flops | bytes accessed | tf_op | source)
XLA Modules:
  0.0 726.6 jit_solution(15192647803113631676)
XLA Ops:
  7.2 0.0 copy-start
  7.2 0.8 copy.58
  8.0 0.1 eq.30
  8.1 0.1 fusion.13
  8.1 0.1 reduce_window_sum.11
  8.2 0.2 select_reduce_fusion
  8.4 0.1 reduce_sum.33
  8.5 0.1 copy.59
  8.5 0.7 multiply_add_fusion
  9.2 0.1 convert_reduce_fusion.1
  9.3 0.0 copy-done
  9.3 0.3 convolution_convert_fusion.1
  9.6 0.9 reshape.47
  10.5 4.8 all-to-all-start.2
  15.3 17.5 %copy.55 = bf16[1,3,128,11008]{2,1,0,3:T(4,128)(2,1)} copy(bf16[1,3,128,11008]{3,2,1,0:T(8,128)(2,1)} %param.6) | data formatting | bytes 16908288 | tf_op args[1]
  32.9 0.0 all-to-all-done.2
  32.9 10.6 %all-to-all-start.1 = ((bf16[1,3,128,11008]{2,1,0,3:T(4,128)(2,1)}), bf16[1,3,128,11008]{2,1,0,3:T(4,128)(2,1)}, u32[]{:S(2)}, u32[]{:S(2)}) async-start(bf16[1,3,128,11008]{2,1,0,3:T(4,128)(2,1)} %copy.55), calls=%async_computation.1 | async-start | bytes 22544384 | tf_op jit(solution)/shard_map/all_to_all | solution.py:41
  43.4 0.1 stack_reshape.2
  43.5 175.2 %all-to-all-done.1 = bf16[1,3,128,11008]{2,1,0,3:T(4,128)(2,1)} async-done(((bf16[1,3,128,11008]{2,1,0,3:T(4,128)(2,1)}), bf16[1,3,128,11008]{2,1,0,3:T(4,128)(2,1)}, u32[]{:S(2)}, u32[]{:S(2)}) %all-to-all-start.1) | async-done | bytes 8454176 | tf_op jit(solution)/shard_map/all_to_all | solution.py:41
  218.7 6.0 stack.3
  224.7 32.5 %all-to-all-start.3 = ((bf16[32,48,4096]{2,1,0:T(8,128)(2,1)}), bf16[32,48,4096]{2,1,0:T(8,128)(2,1)}, u32[]{:S(2)}, u32[]{:S(2)}) async-start(bf16[32,48,4096]{2,1,0:T(8,128)(2,1)} %stack.3), calls=%async_computation.3 | async-start | bytes 25165824 | tf_op jit(solution)/shard_map/all_to_all | solution.py:11
  257.2 0.2 reduce-scatter.4.cloned.1.call-start
  257.5 8.8 %copy.56 = bf16[1,3,128,11008]{2,3,1,0:T(8,128)(2,1)} copy(bf16[1,3,128,11008]{2,1,0,3:T(4,128)(2,1)} %all-to-all-done.1) | data formatting | bytes 16908288 | tf_op jit(solution)/shard_map/all_to_all | solution.py:41
  266.2 9.2 %copy.67 = bf16[1,3,32,43,8,128]{5,4,2,3,1,0:T(8,128)(2,1)} copy(bf16[1,3,32,43,8,128]{5,4,3,2,1,0:T(8,128)(2,1)} %bitcast.33) | data formatting | bytes 16908288 | tf_op jit(solution)/shard_map/all_to_all | solution.py:41
  275.4 171.9 %all-to-all-done.3 = bf16[32,48,4096]{2,1,0:T(8,128)(2,1)} async-done(((bf16[32,48,4096]{2,1,0:T(8,128)(2,1)}), bf16[32,48,4096]{2,1,0:T(8,128)(2,1)}, u32[]{:S(2)}, u32[]{:S(2)}) %all-to-all-start.3) | async-done | bytes 12582944 | tf_op jit(solution)/shard_map/all_to_all | solution.py:11
  447.3 8.5 %fusion.1 = f32[1536,344]{0,1:T(8,128)S(1)} fusion(bf16[1536,4096]{1,0:T(8,128)(2,1)} %bitcast.3, bf16[1,3,4096,344]{2,3,1,0:T(8,128)(2,1)} %bitcast.34), kind=kOutput, calls=%fused_computation.10 | convolution fusion | flops 4328521728 | bytes 17514496 | tf_op jit(solution)/shard_map/dot_general | solution.py:58
  455.8 21.6 %convolution_convert_fusion = bf16[1536,4096]{1,0:T(8,128)(2,1)} fusion(bf16[1,3,4096,344]{2,3,1,0:T(8,128)(2,1)} %bitcast.35, bf16[1536,4096]{1,0:T(8,128)(2,1)} %bitcast.3, f32[1536,344]{0,1:T(8,128)S(1)} %fusion.1), kind=kOutput, calls=%fused_computation | convolution fusion | flops 8666505216 | bytes 32915456 | tf_op jit(solution)/shard_map/dot_general | solution.py:62
  477.4 0.0 reduce-scatter.4.cloned.1.call-update
  477.4 0.0 copy-start.1
  477.4 0.0 reduce-scatter.6.cloned.1.call-start
  477.5 141.7 %reduce-scatter.4.cloned.1.call-done = bf16[384,4096]{1,0:T(8,128)(2,1)} async-done(((bf16[1536,4096]{1,0:T(8,128)(2,1)}), bf16[384,4096]{1,0:T(8,128)(2,1)}) %reduce-scatter.4.cloned.1.call-update) | async-done | bytes 3145744 | tf_op jit(solution)/shard_map/reduce_scatter | solution.py:21
  619.2 0.0 reduce-scatter.6.cloned.1.call-update
  619.2 0.3 reduce-scatter.8.cloned.1.call-start
  619.5 40.1 %reduce-scatter.6.cloned.1.call-done = bf16[96,4096]{1,0:T(8,128)(2,1)} async-done(((bf16[384,4096]{1,0:T(8,128)(2,1)}), bf16[96,4096]{1,0:T(8,128)(2,1)}) %reduce-scatter.6.cloned.1.call-update) | async-done | bytes 786448 | tf_op jit(solution)/shard_map/reduce_scatter | solution.py:21
  659.6 0.0 reduce-scatter.8.cloned.1.call-update
  659.6 0.0 copy-done.1
  659.6 18.1 %copy.54 = bf16[1,2,4096,128]{3,1,0,2:T(2,128)(2,1)} copy(bf16[1,2,4096,128]{3,2,1,0:T(8,128)(2,1)S(1)} %copy-done.1) | data formatting | bytes 4194304 | tf_op args[0]
  677.7 0.0 copy-start.2
  677.7 4.4 all-to-all-start
  682.2 0.1 reduce_sum.35
  682.2 0.0 copy-done.2
  682.3 0.2 fusion.10
  682.4 0.1 copy.60
  682.5 0.1 broadcast_multiply_fusion
  682.6 0.7 reduce-scatter.8.cloned.1.call-done
  683.3 1.9 reshape.49
  685.2 21.7 %all-to-all-done = bf16[1,2,4096,128]{3,1,0,2:T(2,128)(2,1)S(1)} async-done(((bf16[1,2,4096,128]{3,1,0,2:T(2,128)(2,1)}), bf16[1,2,4096,128]{3,1,0,2:T(2,128)(2,1)S(1)}, u32[]{:S(2)}, u32[]{:S(2)}) %all-to-all-start) | async-done | bytes 2097184 | tf_op jit(solution)/shard_map/all_to_all | solution.py:75
  706.9 4.4 all-to-all-start.4
  711.3 2.1 convert_reduce_fusion
  713.4 0.5 multiply_convert_fusion
  713.9 0.9 copy.62
  714.7 4.4 all-to-all-done.4
  719.1 1.0 fusion
Async XLA Ops:
  7.2 2.2 copy-start
  10.5 22.4 %all-to-all-start.2 = ((bf16[4,12,4096]{2,1,0:T(8,128)(2,1)}), bf16[4,12,4096]{2,1,0:T(8,128)(2,1)S(1)}, u32[]{:S(2)}, u32[]{:S(2)}) async-start(bf16[4,12,4096]{2,1,0:T(8,128)(2,1)} %reshape.47), calls=%async_computation.2 | async-start | bytes 1048576 | tf_op jit(solution)/shard_map/all_to_all | solution.py:56
  32.9 185.8 %all-to-all-start.1 = ((bf16[1,3,128,11008]{2,1,0,3:T(4,128)(2,1)}), bf16[1,3,128,11008]{2,1,0,3:T(4,128)(2,1)}, u32[]{:S(2)}, u32[]{:S(2)}) async-start(bf16[1,3,128,11008]{2,1,0,3:T(4,128)(2,1)} %copy.55), calls=%async_computation.1 | async-start | bytes 22544384 | tf_op jit(solution)/shard_map/all_to_all | solution.py:41
  224.7 222.6 %all-to-all-start.3 = ((bf16[32,48,4096]{2,1,0:T(8,128)(2,1)}), bf16[32,48,4096]{2,1,0:T(8,128)(2,1)}, u32[]{:S(2)}, u32[]{:S(2)}) async-start(bf16[32,48,4096]{2,1,0:T(8,128)(2,1)} %stack.3), calls=%async_computation.3 | async-start | bytes 25165824 | tf_op jit(solution)/shard_map/all_to_all | solution.py:11
  257.2 361.9 %reduce-scatter.4.cloned.1.call-start = ((), (), s32[]{:S(2)}) async-start(), calls=%async_computation.8 | async-start | bytes 15728640 | tf_op jit(solution)/shard_map/reduce_scatter | solution.py:21
  477.4 182.2 %copy-start.1 = (bf16[1,2,4096,128]{3,2,1,0:T(8,128)(2,1)S(1)}, bf16[1,2,4096,128]{3,2,1,0:T(8,128)(2,1)}, u32[]{:S(2)}) copy-start(bf16[1,2,4096,128]{3,2,1,0:T(8,128)(2,1)} %param.5) | copy-start | bytes 6291460
  477.4 182.2 %reduce-scatter.6.cloned.1.call-start = ((), (), s32[]{:S(2)}) async-start(), calls=%async_computation.9 | async-start | bytes 3932160 | tf_op jit(solution)/shard_map/reduce_scatter | solution.py:21
  619.2 64.1 %reduce-scatter.8.cloned.1.call-start = ((), (), s32[]{:S(2)}) async-start(), calls=%async_computation.10 | async-start | bytes 1179648 | tf_op jit(solution)/shard_map/reduce_scatter | solution.py:21
  677.7 4.5 copy-start.2
  677.7 29.1 %all-to-all-start = ((bf16[1,2,4096,128]{3,1,0,2:T(2,128)(2,1)}), bf16[1,2,4096,128]{3,1,0,2:T(2,128)(2,1)S(1)}, u32[]{:S(2)}, u32[]{:S(2)}) async-start(bf16[1,2,4096,128]{3,1,0,2:T(2,128)(2,1)} %copy.54), calls=%async_computation | async-start | bytes 4194304 | tf_op jit(solution)/shard_map/all_to_all | solution.py:75
  706.9 12.3 %all-to-all-start.4 = ((bf16[4,12,4096]{2,1,0:T(8,128)(2,1)}), bf16[4,12,4096]{2,1,0:T(8,128)(2,1)S(1)}, u32[]{:S(2)}, u32[]{:S(2)}) async-start(bf16[4,12,4096]{2,1,0:T(8,128)(2,1)} %reshape.49), calls=%async_computation.7 | async-start | bytes 1048576 | tf_op jit(solution)/shard_map/all_to_all | solution.py:68
Sparse Core Ops, SparseCore 0:
  477.5 141.6 reduce-scatter.3
  621.6 37.9 reduce-scatter.5
  661.9 21.3 reduce-scatter.7
